TPU v7x, 16 devices: a whole 2x2x2 slice. The times are simulated.
16 devices in a mesh: tp: 2 (over z), dp: 8 (over y, x, core).
Axes of the slice: x: 2, y: 2, z: 2, core: 2. Of those that a mesh axis runs over, the one named last changes fastest.
Arguments:
- x_saved: bfloat16 [8, 1536, 1024], P('dp', 'tp')
- dy_out: bfloat16 [8, 1536, 1024], P('dp', 'tp')
- ln_params: float32 [4, 1024], replicated
- w_qkv: bfloat16 [1024, 16, 3, 64], P(None, 'tp')
- w_out: bfloat16 [1024, 1024], P('tp')
- w_up: bfloat16 [1024, 4096], P(None, 'tp')
- w_down: bfloat16 [4096, 1024], P('tp')
Outputs:
- output 1: bfloat16 [8, 1536, 1024], P('dp', 'tp')
- output 2: float32 [4, 1024], replicated
- output 3: float32 [1024, 16, 3, 64], P('dp', 'tp')
- output 4: float32 [1024, 1024], P(('tp', 'dp'))
- output 5: float32 [1024, 4096], P('dp', 'tp')
- output 6: float32 [4096, 1024], P(('tp', 'dp'))
All inputs are finite; a program needn't handle non-finite values.
Results may differ from a plain program's by a relative error of at most 0.00985815.
Values are sent between devices in bfloat16 or wider.
A program may use at most 1 GiB of HBM per device.

v0:
```python
import functools

import jax
import jax.numpy as jnp
from jax import lax
from jax.experimental import pallas as pl
from jax.experimental.pallas import tpu as pltpu
from jax.sharding import PartitionSpec as P

NORM_EPS = 1e-5
ROPE_BASE = 10000.0
BF = jnp.bfloat16
F32 = jnp.float32
SQRT_HALF = 0.7071067811865476
INV_SQRT_2PI = 0.3989422804014327
VMEM_LIMIT = 60 * 1024 * 1024


def dot(a, b, ca, cb):
    return lax.dot_general(a, b, (((ca,), (cb,)), ((), ())), preferred_element_type=F32)


def params():
    return pltpu.CompilerParams(vmem_limit_bytes=VMEM_LIMIT)


def cost(flops, nbytes, trans=0):
    return pl.CostEstimate(flops=int(flops), bytes_accessed=int(nbytes), transcendentals=int(trans))


def normalized(x):
    cen = x - jnp.mean(x, axis=-1, keepdims=True)
    rstd = lax.rsqrt(jnp.mean(cen * cen, axis=-1, keepdims=True) + NORM_EPS)
    return cen * rstd, rstd


def norm_m_kernel(c_ref, x_ref, ln_ref, hm_ref, hk_ref, hs_ref):
    hm = (normalized(x_ref[...].astype(F32))[0] * ln_ref[2:3, :] + ln_ref[3:4, :]).astype(BF)
    hm_ref[...] = hm
    n = hm.shape[1] // 8
    for j in range(4):
        even, odd = hm[:, 2 * j * n:(2 * j + 1) * n].T, hm[:, (2 * j + 1) * n:(2 * j + 2) * n].T
        hk_ref[j * n:(j + 1) * n, :] = jnp.where(c_ref[0] == 0, even, odd)
        hs_ref[j * n:(j + 1) * n, :] = jnp.where(c_ref[0] == 0, odd, even)


def norm_m(core, x, ln, bt=256):
    rows, d = x.shape
    tok = pl.BlockSpec((bt, d), lambda i, c: (i, 0))
    return pl.pallas_call(
        norm_m_kernel,
        grid_spec=pltpu.PrefetchScalarGridSpec(
            num_scalar_prefetch=1,
            grid=(rows // bt,),
            in_specs=[tok, pl.BlockSpec((4, d), lambda i, c: (0, 0))],
            out_specs=[tok] + [pl.BlockSpec((d // 2, bt), lambda i, c: (0, i))] * 2,
        ),
        out_shape=[jax.ShapeDtypeStruct((rows, d), BF)] + [jax.ShapeDtypeStruct((d // 2, rows), BF)] * 2,
        compiler_params=params(),
        cost_estimate=cost(3e9, rows * d * 6),
        name="norm_m",
    )(core, x, ln)


def norm_a_kernel(c_ref, xl_ref, xr_ref, ln_ref, ha_ref, hk_ref, hs_ref, *, nb):
    def run(x_ref):
        ha = (normalized(x_ref[...].astype(F32))[0] * ln_ref[0:1, :] + ln_ref[1:2, :]).astype(BF)
        ha_ref[...] = ha
        n = ha.shape[1] // 8
        for j in range(4):
            even, odd = ha[:, 2 * j * n:(2 * j + 1) * n], ha[:, (2 * j + 1) * n:(2 * j + 2) * n]
            hk_ref[:, j * n:(j + 1) * n] = jnp.where(c_ref[0] == 0, even, odd)
            hs_ref[:, j * n:(j + 1) * n] = jnp.where(c_ref[0] == 0, odd, even)

    pl.when(pl.program_id(0) < nb)(lambda: run(xl_ref))
    pl.when(pl.program_id(0) >= nb)(lambda: run(xr_ref))


def norm_a(core, x_loc, x_rem, ln, bt=256):
    rows, d = x_loc.shape
    nb = rows // bt
    tok = lambda w: pl.BlockSpec((bt, w), lambda i, c: (i, 0))
    return pl.pallas_call(
        functools.partial(norm_a_kernel, nb=nb),
        grid_spec=pltpu.PrefetchScalarGridSpec(
            num_scalar_prefetch=1,
            grid=(2 * nb,),
            in_specs=[
                pl.BlockSpec((bt, d), lambda i, c: (jnp.minimum(i, nb - 1), 0)),
                pl.BlockSpec((bt, d), lambda i, c: (jnp.maximum(i - nb, 0), 0)),
                pl.BlockSpec((4, d), lambda i, c: (0, 0)),
            ],
            out_specs=[tok(d), tok(d // 2), tok(d // 2)],
        ),
        out_shape=[jax.ShapeDtypeStruct((2 * rows, w), BF) for w in (d, d // 2, d // 2)],
        compiler_params=params(),
        cost_estimate=cost(6e9, rows * d * 12),
        name="norm_a",
    )(core, x_loc, x_rem, ln)


MESH = pl.DeviceIdType.MESH


def partners():
    me, t = lax.axis_index("dp"), lax.axis_index("tp")
    c, xx, yy = me % 2, (me // 2) % 2, me // 4
    way = {"c": {"dp": me + 1 - 2 * c}, "x": {"dp": me + 2 - 4 * xx}, "y": {"dp": me + 4 - 8 * yy}, "z": {"tp": 1 - t}}
    return way, t, c, xx, yy


def meet(way, names):
    barrier = pltpu.get_barrier_semaphore()
    for p in names:
        pl.semaphore_signal(barrier, inc=1, device_id=way[p], device_id_type=MESH)
    pl.semaphore_wait(barrier, len(names))


def by_rows(n, chunk, f):
    def body(i, _):
        f(pl.ds(pl.multiple_of(i * chunk, 8), chunk))
        return _

    lax.fori_loop(0, n // chunk, body, 0)


WAYS = ("x", "y"), ("y", "x")


def attn_kernel(qkv_ref, dol_ref, dor_ref, cos_ref, sin_ref,
                d_out, d_stay, uka, ukb, usa, usb,
                dqkv_ref, ctx_ref, gd_ref, us_ref, uk_ref,
                dk_ref, dv_ref, d_keep, u_keep, u_got, d1_got, u1_send, u1_got, d2_send, d2_got,
                load_sem, send_sem, recv_sem, *, bq, hd):
    way, t, _, xx, yy = partners()
    step = pl.program_id(0)
    last = pl.num_programs(0) - 1

    def remote(i, src, dst, w):
        return pltpu.make_async_remote_copy(
            src_ref=src, dst_ref=dst, send_sem=send_sem.at[i], recv_sem=recv_sem.at[i], device_id=way[w], device_id_type=MESH)

    core_u = [remote(2 + k, src, u_got.at[k], "c") for k, src in enumerate((usa, usb))]
    first_d = [remote(k, d_out.at[k], d1_got.at[k], WAYS[k][0]) for k in range(2)]
    second_d = [remote(4 + k, d2_send.at[k], d2_got.at[k], WAYS[k][1]) for k in range(2)]
    first_u = [remote(6 + k, u1_send.at[k], u1_got.at[k], WAYS[k][0]) for k in range(2)]
    load_d = pltpu.make_async_copy(d_stay, d_keep, load_sem.at[0])
    load_u = [pltpu.make_async_copy(src, u_keep.at[k], load_sem.at[2 + k]) for k, src in enumerate((uka, ukb))]

    leave = [lambda i: 2 * i + 1 - xx, lambda i: 2 * (1 - yy) + i]
    stay = [lambda i: 2 * i + xx, lambda i: 2 * yy + i]
    mine = [yy, xx]

    @pl.when(step == 0)
    def _():
        meet(way, "cxy")
        for v in first_d + core_u + [load_d] + load_u:
            v.start()

    @pl.when(step == 3)
    def _():
        for k in range(2):
            load_u[k].wait()
            core_u[k].wait()
            for i in range(2):
                def add(r):
                    for j in range(u_keep.shape[1]):
                        u1_send[k, i, j, r, :] = u_keep[k, j, leave[k](i), r, :] + u_got[k, j, leave[k](i), r, :]
                        u_keep[k, j, stay[k](i), r, :] += u_got[k, j, stay[k](i), r, :]

                by_rows(u_keep.shape[3], 16, add)
            first_u[k].start()

    @pl.when(step == 4)
    def _():
        load_d.wait()
        for k in range(2):
            first_d[k].wait()
            m = mine[k]

            def add(r):
                d2_send[k, r, :] = d_keep[k, 1 - m, r, :] + d1_got[k, 1 - m, r, :]
                d_keep[k, m, r, :] += d1_got[k, m, r, :]

            by_rows(d_keep.shape[2], 32, add)
            second_d[k].start()

    @pl.when(step == last)
    def _():
        for k in range(2):
            first_u[k].wait()
            m = mine[k]

            def add(r):
                for j in range(u_keep.shape[1]):
                    us_ref[k, j, r, :] = u_keep[k, j, stay[k](1 - m), r, :] + u1_got[k, 1 - m, j, r, :]
                    uk_ref[k, j, r, :] = u_keep[k, j, stay[k](m), r, :] + u1_got[k, m, j, r, :]

            by_rows(u_keep.shape[3], 16, add)

    attn_head(t, qkv_ref, dol_ref, dor_ref, cos_ref, sin_ref, dqkv_ref, ctx_ref, dk_ref, dv_ref, bq, hd)

    @pl.when(step == last)
    def _():
        w = d_keep.shape[3]
        for k in range(2):
            second_d[k].wait()
            m = mine[k]

            def add(r):
                gd_ref[r, k * w:(k + 1) * w] = d_keep[k, m, r, :] + d2_got[k, r, :]

            by_rows(d_keep.shape[2], 32, add)


def attn_head(t, qkv_ref, dol_ref, dor_ref, cos_ref, sin_ref, dqkv_ref, ctx_ref, dk_ref, dv_ref, bq, hd):
    seq = qkv_ref.shape[1]
    half = hd // 2
    part = dol_ref.shape[1]
    cos, sin = cos_ref[...], sin_ref[...]

    def in_order(own, peer):
        return jnp.concatenate([jnp.where(t == 0, own, peer), jnp.where(t == 0, peer, own)], axis=1)

    def place(lo, n):
        slot = t if lo < part else 1 - t
        return pl.ds(pl.multiple_of(slot * part + lo % part, 128), n)

    def rope(v):
        lo, hi = v[:half].astype(F32), v[half:].astype(F32)
        return jnp.concatenate([lo * cos - hi * sin, hi * cos + lo * sin], axis=0).astype(BF)

    def rope_back(d, c, s):
        lo, hi = d[:half].astype(BF).astype(F32), d[half:].astype(BF).astype(F32)
        return jnp.concatenate([lo * c + hi * s, hi * c - lo * s], axis=0).astype(BF)

    scale = hd ** -0.5
    qkv = in_order(qkv_ref[:, :part], qkv_ref[:, part:])
    q_t = rope(qkv[0:hd])
    k_t = rope(qkv[hd:2 * hd])
    v_t = qkv[2 * hd:3 * hd]
    q_t = (q_t.astype(F32) * scale).astype(BF)
    do_t = in_order(dol_ref[...], dor_ref[...])
    q_n, do_n, k_n, v_n = q_t.T, do_t.T, k_t.T, v_t.T
    tri = lax.broadcasted_iota(jnp.int32, (bq, bq), 0) <= lax.broadcasted_iota(jnp.int32, (bq, bq), 1)
    for i in range(seq // bq):
        lo, nk = i * bq, (i + 1) * bq
        blocks = [slice(j * bq, (j + 1) * bq) for j in range(i + 1)]
        q_b, do_b = q_t[:, lo:nk], do_t[:, lo:nk]
        ss = [dot(k_n[b], q_b, 1, 0) for b in blocks]
        ss[i] = jnp.where(tri, ss[i], -1e30)
        m = functools.reduce(jnp.maximum, [jnp.max(s, axis=0, keepdims=True) for s in ss])
        es = [jnp.exp(s - m) for s in ss]
        r = 1.0 / sum(jnp.sum(e, axis=0, keepdims=True) for e in es)
        ps = [e * r for e in es]
        pbs = [p.astype(BF) for p in ps]
        dps = [dot(v_n[b], do_b, 1, 0).astype(BF) for b in blocks]
        delta = sum(jnp.sum(p * d.astype(F32), axis=0, keepdims=True) for p, d in zip(ps, dps))
        dss = [(p * (d.astype(F32) - delta)).astype(BF) for p, d in zip(ps, dps)]
        ctx_ref[:, place(lo, bq)] = sum(dot(v_t[:, b], p, 1, 0) for b, p in zip(blocks, pbs)).astype(BF)
        dq = sum(dot(k_t[:, b], d, 1, 0) for b, d in zip(blocks, dss)) * scale
        dqkv_ref[0:hd, place(lo, bq)] = rope_back(dq, cos[:, lo:nk], sin[:, lo:nk])
        for j, b in enumerate(blocks):
            dv_new = dot(pbs[j], do_n[lo:nk], 1, 0)
            dk_new = dot(dss[j], q_n[lo:nk], 1, 0)
            if j < i:
                dv_ref[b, :] += dv_new
                dk_ref[b, :] += dk_new
            else:
                dv_ref[b, :] = dv_new
                dk_ref[b, :] = dk_new
    dk = rope_back(dk_ref[...].T, cos, sin)
    dv = dv_ref[...].T.astype(BF)
    for lo in (0, part):
        dqkv_ref[hd:2 * hd, place(lo, part)] = dk[:, lo:lo + part]
        dqkv_ref[2 * hd:3 * hd, place(lo, part)] = dv[:, lo:lo + part]


def attention(qkv_t, dol, dor, cos_t, sin_t, down, up, hd, bq=256):
    rows, seq = qkv_t.shape
    heads = rows // (3 * hd)
    part = dol.shape[1]
    const = pl.BlockSpec((hd // 2, seq), lambda g: (0, 0))
    row = lambda r, w: pl.BlockSpec((r, w), lambda g: (g, 0))
    hbm = pl.BlockSpec(memory_space=pl.ANY)
    dsh, ush = down[0].shape, up[0].shape
    dred, ured = dsh[2:], (ush[0],) + ush[2:]
    gd_shape = (dred[0], 2 * dred[1])
    whole = lambda *shape: pl.BlockSpec(shape, lambda g: (0,) * len(shape))
    f = lambda *shape: pltpu.VMEM(shape, F32)
    sds = jax.ShapeDtypeStruct
    return pl.pallas_call(
        functools.partial(attn_kernel, bq=bq, hd=hd),
        grid=(heads,),
        in_specs=[row(3 * hd, seq), row(hd, part), row(hd, part), const, const] + [hbm] * 6,
        out_specs=[row(3 * hd, seq), row(hd, seq), whole(*gd_shape), whole(2, *ured), whole(2, *ured)],
        out_shape=[sds((rows, seq), BF), sds((heads * hd, seq), BF), sds(gd_shape, F32), sds((2,) + ured, F32), sds((2,) + ured, F32)],
        scratch_shapes=[
            f(seq, hd), f(seq, hd), f(*dsh), f(2, *ush), f(2, *ush),
            f(*dsh), f(2, 2, *ured), f(2, 2, *ured), f(2, *dred), f(2, *dred),
            pltpu.SemaphoreType.DMA((4,)), pltpu.SemaphoreType.DMA((10,)), pltpu.SemaphoreType.DMA((10,)),
        ],
        compiler_params=pltpu.CompilerParams(vmem_limit_bytes=VMEM_LIMIT, collective_id=1, has_side_effects=True),
        cost_estimate=cost(heads * 6e9, heads << 20, seq * seq * heads // 2),
        name="attn",
    )(qkv_t, dol, dor, cos_t, sin_t, *down, *up)


def gelu_pair(h_ref, dy_ref, wu, wd, rows):
    u = dot(h_ref[rows, :], wu, 1, 0).astype(BF).astype(F32)
    dg = dot(dy_ref[rows, :], wd, 1, 1).astype(BF).astype(F32)
    cdf = 0.5 + 0.5 * lax.erf(u * SQRT_HALF)
    pdf = jnp.exp(-0.5 * u * u) * INV_SQRT_2PI
    return (u * cdf).astype(BF), (dg * (cdf + u * pdf)).astype(BF)


def mlp_own_kernel(h_ref, dy_ref, wu_ref, wd_ref, at_ref, du_ref, dh_ref, acc_ref, *, tc):
    step = pl.program_id(0)
    wu, wd = wu_ref[...], wd_ref[...]
    for k in range(h_ref.shape[0] // tc):
        rows = pl.ds(k * tc, tc)
        a, du = gelu_pair(h_ref, dy_ref, wu, wd, rows)
        at_ref[:, rows] = a.T
        du_ref[0, rows, :] = du
        add = dot(du, wu, 1, 1)

        @pl.when(step == 0)
        def _():
            acc_ref[rows, :] = add

        @pl.when(step > 0)
        def _():
            acc_ref[rows, :] += add

    @pl.when(step == pl.num_programs(0) - 1)
    def _():
        dh_ref[...] = acc_ref[...].astype(BF)


def mlp_own(h, dy, w_up, w_down, n=4, tc=256):
    seq, d = h.shape
    ff = w_up.shape[1]
    fb = ff // n
    full = pl.BlockSpec((seq, d), lambda i: (0, 0))
    return pl.pallas_call(
        functools.partial(mlp_own_kernel, tc=tc),
        grid=(n,),
        in_specs=[full, full, pl.BlockSpec((d, fb), lambda i: (0, i)), pl.BlockSpec((fb, d), lambda i: (i, 0))],
        out_specs=[pl.BlockSpec((fb, seq), lambda i: (i, 0)), pl.BlockSpec((1, seq, fb), lambda i: (i, 0, 0)), full],
        out_shape=[jax.ShapeDtypeStruct((ff, seq), BF), jax.ShapeDtypeStruct((n, seq, fb), BF), jax.ShapeDtypeStruct((seq, d), BF)],
        scratch_shapes=[pltpu.VMEM((seq, d), F32)],
        compiler_params=params(),
        cost_estimate=cost(6 * seq * d * ff, 20 << 20, 2 * seq * ff),
        name="mlp_own",
    )(h, dy, w_up, w_down)


def mlp_pre_kernel(h_ref, wu_ref, at_ref, gp_ref, *, tc):
    wu = wu_ref[...]
    for k in range(h_ref.shape[0] // tc):
        rows = pl.ds(k * tc, tc)
        u = dot(h_ref[rows, :], wu, 1, 0).astype(BF).astype(F32)
        cdf = 0.5 + 0.5 * lax.erf(u * SQRT_HALF)
        pdf = jnp.exp(-0.5 * u * u) * INV_SQRT_2PI
        at_ref[:, rows] = (u * cdf).astype(BF).T
        gp_ref[0, rows, :] = cdf + u * pdf


def mlp_pre(h, w_up, n=4, tc=256):
    seq, d = h.shape
    ff = w_up.shape[1]
    fb = ff // n
    return pl.pallas_call(
        functools.partial(mlp_pre_kernel, tc=tc),
        grid=(n,),
        in_specs=[pl.BlockSpec((seq, d), lambda i: (0, 0)), pl.BlockSpec((d, fb), lambda i: (0, i))],
        out_specs=[pl.BlockSpec((fb, seq), lambda i: (i, 0)), pl.BlockSpec((1, seq, fb), lambda i: (i, 0, 0))],
        out_shape=[jax.ShapeDtypeStruct((ff, seq), BF), jax.ShapeDtypeStruct((n, seq, fb), F32)],
        compiler_params=params(),
        cost_estimate=cost(2 * seq * d * ff, 16 << 20, 2 * seq * ff),
        name="mlp_pre",
    )(h, w_up)


def mlp_peer_kernel(dyr_ref, dyl_ref, hkl_ref, hsl_ref, hkr_ref, hsr_ref, wu_ref, wd_ref, wo_ref, at_ref, atr_ref, dul_ref, gp_ref,
                    d_out, d_stay, uka_ref, ukb_ref, usa_ref, usb_ref, dh_ref, dctx_ref,
                    acc_ref, du_ref, d_keep, d_send, d_got, send_sem, recv_sem, *, tc):
    way, _, c, xx, yy = partners()
    step = pl.program_id(0)
    last = pl.num_programs(0) - 1
    wu, wd = wu_ref[...], wd_ref[...]
    fb = wu.shape[1]
    m = fb // 2

    def remote(i):
        return pltpu.make_async_remote_copy(
            src_ref=d_send.at[i], dst_ref=d_got.at[i], send_sem=send_sem.at[i], recv_sem=recv_sem.at[i],
            device_id=way["c"], device_id_type=MESH)

    def combine(i):
        remote(i).wait()
        y, x = i // 2, i % 2
        for k, at, go in ((0, y, x != xx), (1, x, y != yy)):
            for ref, cond in ((d_out, go), (d_stay, jnp.logical_not(go))):
                @pl.when(cond)
                def _():
                    def add(r):
                        ref[k, at, r, :] = d_keep[i, k, r, :] + d_got[i, k, r, :]

                    by_rows(m, 32, add)

    pl.when(step == 0)(lambda: meet(way, "c"))
    dctx_ref[...] = dot(wo_ref[...], dyr_ref[...], 1, 1).astype(BF)

    @pl.when(step == 0)
    def _():
        acc_ref[...] = jnp.zeros_like(acc_ref)

    for k in range(dyr_ref.shape[0] // tc):
        rows = pl.ds(k * tc, tc)
        dg = dot(dyr_ref[rows, :], wd, 1, 1).astype(BF).astype(F32)
        du = (dg * gp_ref[0, rows, :]).astype(BF)
        du_ref[rows, :] = du
        acc_ref[rows, :] += dot(du, wu, 1, 1)
    for side, ref in ((1 - c, d_send), (c, d_keep)):
        block = pl.ds(pl.multiple_of(side * m, 128), m)
        g = dot(at_ref[block, :], dyl_ref[...], 1, 0) + dot(atr_ref[block, :], dyr_ref[...], 1, 0)
        w = g.shape[1] // 2
        ref[step, 0] = g[:, :w]
        ref[step, 1] = g[:, w:]
        if ref is d_send:
            remote(step).start()
    for hl, hr, ra, rb in ((hkl_ref, hkr_ref, uka_ref, ukb_ref), (hsl_ref, hsr_ref, usa_ref, usb_ref)):
        g = dot(hl[...], dul_ref[0], 1, 0) + dot(hr[...], du_ref[...], 1, 0)
        n = g.shape[0] // 4
        for j in range(4):
            ra[0, j] = g[j * n:(j + 1) * n, :m]
            rb[0, j] = g[j * n:(j + 1) * n, m:]

    pl.when(step > 0)(lambda: combine(step - 1))

    @pl.when(step == last)
    def _():
        combine(step)
        dh_ref[...] = acc_ref[...].astype(BF)


def mlp_peer(dy_rem, dy_loc, hts, w_up, w_down, w_out, at, at_rem, du, slope, n=4, tc=256):
    seq, d = dy_rem.shape
    ff = w_up.shape[1]
    fb = ff // n
    ctx = w_out.shape[0]
    full = lambda r, w: pl.BlockSpec((r, w), lambda i: (0, 0))
    rows = lambda r, w: pl.BlockSpec((r, w), lambda i: (i, 0))
    dshape = (2, 2, fb // 2, d // 2)
    dspec = pl.BlockSpec(dshape, lambda i: (0, 0, 0, 0))
    uspec = pl.BlockSpec((1, 4, d // 8, fb // 2), lambda i: (i, 0, 0, 0))
    act = pl.BlockSpec((1, seq, fb), lambda i: (i, 0, 0))
    sds = jax.ShapeDtypeStruct
    slots = pltpu.VMEM((n, 2, fb // 2, d // 2), F32)
    return pl.pallas_call(
        functools.partial(mlp_peer_kernel, tc=tc),
        grid=(n,),
        in_specs=[full(seq, d)] * 2 + [full(d // 2, seq)] * 4 + [
            pl.BlockSpec((d, fb), lambda i: (0, i)), rows(fb, d), rows(ctx // n, d), rows(fb, seq), rows(fb, seq), act, act],
        out_specs=[dspec] * 2 + [uspec] * 4 + [full(seq, d), rows(ctx // n, seq)],
        out_shape=[sds(dshape, F32)] * 2 + [sds((n, 4, d // 8, fb // 2), F32)] * 4 + [sds((seq, d), BF), sds((ctx, seq), BF)],
        scratch_shapes=[pltpu.VMEM((seq, d), F32), pltpu.VMEM((seq, fb), BF), slots, slots, slots,
                        pltpu.SemaphoreType.DMA((n,)), pltpu.SemaphoreType.DMA((n,))],
        compiler_params=pltpu.CompilerParams(vmem_limit_bytes=63 * 1024 * 1024, collective_id=2, has_side_effects=True),
        cost_estimate=cost(14 * seq * d * ff, 40 << 20),
        name="mlp_peer",
    )(dy_rem, dy_loc, *hts, w_up, w_down, w_out, at, at_rem, du, slope)


def tail_kernel(*refs, bt, hd):
    n_in = 13
    hbm, us_ref, refs = refs[:n_in], refs[n_in], refs[n_in + 1:]
    (gx_ref, sums_ref, gq_ref, gw_ref, gu_ref), refs = refs[:5], refs[5:]
    vm, refs = refs[:n_in], refs[n_in:]
    (z_send, z_recv, sum_src, sum_got, q_keep, q_send, q_recv, w_keep, w_send, w_recv,
     q1_send, q1_recv, w1_send, w1_recv, q2_send, q2_recv, w2_send, w2_recv, u2_recv,
     in_sem, send_sem, recv_sem) = refs
    dq, ctx, hk, hs, wt, xl, xr, dhl, dhr, dyl, dyr, ln, uk = vm
    way_to, t, c, xx, yy = partners()
    part = xl.shape[0]
    gr = dq.shape[0] // 4

    loads = [pltpu.make_async_copy(src, dst, in_sem.at[i]) for i, (src, dst) in enumerate(zip(hbm, vm))]
    for i in (0, 4, 6, 8, 11, 3, 2, 1, 9, 10, 5, 7, 12):
        loads[i].start()
    meet(way_to, "cxyz")

    count = [0]

    def send(src, dst, way):
        i = count[0]
        count[0] += 1
        copy = pltpu.make_async_remote_copy(
            src_ref=src, dst_ref=dst, send_sem=send_sem.at[i], recv_sem=recv_sem.at[i],
            device_id=way_to[way], device_id_type=MESH)
        copy.start()
        return copy

    def need(*idx):
        for i in idx:
            loads[i].wait()

    def block(x_ref, dh_ref, b, peer):
        rows = pl.ds(b * bt, bt)
        cols = pl.ds((part if peer else 0) + b * bt, bt)
        dha = dot(dq[:, cols], wt[...], 0, 0).astype(BF).astype(F32)
        dhm = dh_ref[rows, :].astype(F32)
        xh, rstd = normalized(x_ref[rows, :].astype(F32))
        dxh = (dha * ln[0:1, :] + dhm * ln[2:3, :]).astype(BF)
        parts = [dha * xh, dha, dhm * xh, dhm]
        return dxh, jnp.concatenate([jnp.sum(p, axis=0, keepdims=True) for p in parts], axis=0)

    def peer_block(b):
        dxh, s = block(xr, dhr, b, True)
        z_send[b] = dxh
        if b == 0:
            sum_src[0] = s
        else:
            sum_src[0] += s
        return send(z_send.at[b], z_recv.at[b], "z")

    def looped(start, n, f):
        def body(i, _):
            f(i)
            return _

        lax.fori_loop(start, start + n, body, 0)

    def qkv_grad(h_ref, out_ref, g):
        r = dot(dq[pl.ds(pl.multiple_of(g * gr, 128), gr), :], h_ref[...], 1, 0)
        n = r.shape[1] // 4
        for j in range(4):
            out_ref[g, j] = r[:, j * n:(j + 1) * n]

    def out_grad(want, out_ref):
        cx = jnp.concatenate([jnp.where(want == 0, ctx[2 * j * hd:(2 * j + 1) * hd, :], ctx[(2 * j + 1) * hd:(2 * j + 2) * hd, :])
                              for j in range(4)], axis=0)
        r = dot(cx[:, :part], dyl[...], 1, 0) + dot(cx[:, part:], dyr[...], 1, 0)
        m = r.shape[1] // 2
        for j in range(4):
            for k in range(2):
                out_ref[k, j] = r[j * hd:(j + 1) * hd, k * m:(k + 1) * m]

    def first(keep, got, out, k):
        for i in range(2):
            s_idx = 2 * i + 1 - xx if k == 0 else 2 * (1 - yy) + i
            k_idx = 2 * i + xx if k == 0 else 2 * yy + i
            out[i] = keep[s_idx] + got[s_idx]
            got[k_idx] = keep[k_idx] + got[k_idx]

    def second(got, got1, out, k):
        mine, other = (yy, 1 - yy) if k == 0 else (xx, 1 - xx)
        at = (lambda i: 2 * i + xx) if k == 0 else (lambda i: 2 * yy + i)
        out[...] = got[at(other)] + got1[other]
        return got[at(mine)] + got1[mine]

    ways = ("x", "y"), ("y", "x")

    us = [send(us_ref.at[k], u2_recv.at[k], ways[k][1]) for k in range(2)]
    need(0, 4, 6, 8, 11)
    zs = [peer_block(0)]
    q1, q2 = [None] * 4, [None] * 4
    n = gq_ref.shape[0] // 4

    def q_first(g):
        first(q_keep.at[g], q_recv.at[g], q1_send.at[g], g % 2)
        q1[g] = send(q1_send.at[g], q1_recv.at[g], ways[g % 2][0])

    def q_second(g):
        q1[g].wait()
        gq_ref[g * n:(g + 1) * n, :] = second(q_recv.at[g], q1_recv.at[g], q2_send.at[g], g % 2)
        q2[g] = send(q2_send.at[g], q2_recv.at[g], ways[g % 2][1])

    need(3)
    for g in (0, 2):
        looped(g, 2, lambda i: qkv_grad(hs, q_send, i))
        qc = send(q_send.at[pl.ds(g, 2)], q_recv.at[pl.ds(g, 2)], "c")
        if g == 0:
            need(2)
        else:
            zs.append(peer_block(1))
        looped(g, 2, lambda i: qkv_grad(hk, q_keep, i))
        qc.wait()
        q_first(g)
        q_first(g + 1)
    zs.append(peer_block(2))
    q_second(0)
    q_second(1)
    need(1, 9, 10)
    out_grad(1 - c, w_send)
    wc = send(w_send, w_recv, "c")
    out_grad(c, w_keep)
    wc.wait()
    w1 = []
    for k in range(2):
        first(w_keep.at[k], w_recv.at[k], w1_send.at[k], k)
        w1.append(send(w1_send.at[k], w1_recv.at[k], ways[k][0]))

    need(5, 7)

    def own_block(b):
        dxh, s = block(xl, dhl, b, False)
        gx_ref[pl.ds(b * bt, bt), :] = dxh
        sum_src[0] += s

    def grad_x(b):
        zs[b].wait()
        rows = pl.ds(b * bt, bt)
        dxh = gx_ref[rows, :].astype(F32) + z_recv[b].astype(F32)
        xh, rstd = normalized(xl[rows, :].astype(F32))
        dx = rstd * (dxh - jnp.mean(dxh, -1, keepdims=True) - xh * jnp.mean(dxh * xh, -1, keepdims=True))
        gx_ref[rows, :] = (dyl[rows, :].astype(F32) + dx).astype(BF)

    own_block(0)
    q_second(2)
    q_second(3)
    own_block(1)
    grad_x(0)
    own_block(2)
    sums = [send(sum_src.at[0], sum_got.at[0], "z")]
    grad_x(1)

    def sum_next(i, way):
        sums[-1].wait()
        sum_src[i] = sum_src[i - 1] + sum_got[i - 1]
        sums.append(send(sum_src.at[i], sum_got.at[i], way))

    sum_next(1, "c")
    need(12)
    blocks, m = uk.shape[1], uk.shape[3]
    for k in range(2):
        us[k].wait()
        for j in range(blocks):
            gu_ref[:, (2 * j + k) * m:(2 * j + k + 1) * m] = uk[k, j] + u2_recv[k, j]
    m = gw_ref.shape[1] // 2
    w2 = []
    for k in range(2):
        w1[k].wait()
        gw_ref[:, k * m:(k + 1) * m] = second(w_recv.at[k], w1_recv.at[k], w2_send.at[k], k)
        w2.append(send(w2_send.at[k], w2_recv.at[k], ways[k][1]))
    sum_next(2, "x")
    for g in (0, 1):
        q2[g].wait()
        gq_ref[g * n:(g + 1) * n, :] += q2_recv[g]
    sum_next(3, "y")
    for g in (2, 3):
        q2[g].wait()
        gq_ref[g * n:(g + 1) * n, :] += q2_recv[g]
    for k in range(2):
        w2[k].wait()
        gw_ref[:, k * m:(k + 1) * m] += w2_recv[k]
    sums[-1].wait()
    sums_ref[...] = sum_src[3] + sum_got[3]
    grad_x(2)


def tail(dq, ctx, h_keep, h_send, w_t, x_loc, x_rem, dhm_loc, dhm_rem, dy_loc, dy_rem, ln, u_keep, u_send, hd, bt=256):
    ins = [dq, ctx, h_keep, h_send, w_t, x_loc, x_rem, dhm_loc, dhm_rem, dy_loc, dy_rem, ln, u_keep]
    part, d = x_loc.shape
    rows = dq.shape[0] // 4
    nb = part // bt
    cols = d // 8
    f = lambda *shape: pltpu.VMEM(shape, F32)
    sds = jax.ShapeDtypeStruct
    scratch = [pltpu.VMEM(v.shape, v.dtype) for v in ins] + [
        pltpu.VMEM((nb, bt, d), BF), pltpu.VMEM((nb, bt, d), BF), f(4, 4, d), f(4, 4, d),
        f(4, 4, rows, cols), f(4, 4, rows, cols), f(4, 4, rows, cols),
        f(2, 4, hd, d // 2), f(2, 4, hd, d // 2), f(2, 4, hd, d // 2),
        f(4, 2, rows, cols), f(4, 2, rows, cols), f(2, 2, hd, d // 2), f(2, 2, hd, d // 2),
        f(4, rows, cols), f(4, rows, cols), f(2, hd, d // 2), f(2, hd, d // 2), f(*u_send.shape),
        pltpu.SemaphoreType.DMA((len(ins),)), pltpu.SemaphoreType.DMA((32,)), pltpu.SemaphoreType.DMA((32,)),
    ]
    vm = pl.BlockSpec(memory_space=pltpu.VMEM)
    u_cols = u_keep.shape[0] * u_keep.shape[1] * u_keep.shape[3]
    return pl.pallas_call(
        functools.partial(tail_kernel, bt=bt, hd=hd),
        in_specs=[pl.BlockSpec(memory_space=pl.ANY)] * (len(ins) + 1),
        out_specs=[vm] * 5,
        out_shape=[sds((part, d), BF), sds((4, d), F32), sds((4 * rows, cols), F32), sds((hd, d), F32), sds((u_keep.shape[2], u_cols), F32)],
        scratch_shapes=scratch,
        compiler_params=pltpu.CompilerParams(vmem_limit_bytes=VMEM_LIMIT, collective_id=0, has_side_effects=True),
        cost_estimate=cost(4e10, 40 << 20),
        name="tail",
    )(*ins, u_send)


def emit_kernel(*refs, n):
    ins, outs, bufs, (sem_in, sem_out) = refs[:n], refs[n:2 * n], refs[2 * n:3 * n], refs[3 * n:]
    get = [pltpu.make_async_copy(ins[i], bufs[i], sem_in.at[i]) for i in range(n)]
    put = [pltpu.make_async_copy(bufs[i], outs[i], sem_out.at[i]) for i in range(n)]
    for v in get:
        v.start()
    for i in range(n):
        get[i].wait()
        put[i].start()
    for v in put:
        v.wait()


def emit(*arrays):
    n = len(arrays)
    hbm = pl.BlockSpec(memory_space=pl.ANY)
    return pl.pallas_call(
        functools.partial(emit_kernel, n=n),
        in_specs=[hbm] * n,
        out_specs=[hbm] * n,
        out_shape=[jax.ShapeDtypeStruct(v.shape, v.dtype) for v in arrays],
        scratch_shapes=[pltpu.VMEM(v.shape, v.dtype) for v in arrays]
        + [pltpu.SemaphoreType.DMA((n,)), pltpu.SemaphoreType.DMA((n,))],
        compiler_params=params(),
        cost_estimate=cost(1e6, 10 << 20),
        name="emit",
    )(*arrays)


def solution(mesh):
    dp = mesh.shape["dp"]
    tp = mesh.shape["tp"]

    def swap_tp(v):
        return lax.ppermute(v, "tp", [(i, i ^ 1) for i in range(tp)])

    def after(v, *deps):
        return lax.optimization_barrier((v,) + deps)[0]

    def local_step(x_loc, dy_loc, ln_params, w_qkv, w_out, w_up, w_down):
        x_loc, dy_loc = x_loc[0], dy_loc[0]
        half, d = x_loc.shape
        seq = half * tp
        heads, hd = w_qkv.shape[1], w_qkv.shape[3]
        me = lax.axis_index("dp")
        c1 = (me % 2).astype(jnp.int32)[None]

        x_rem = swap_tp(x_loc)
        dy_rem = swap_tp(dy_loc)

        w_t = w_qkv.transpose(1, 2, 3, 0).reshape(heads * 3 * hd, d)
        inv_freq = ROPE_BASE ** (-2.0 * jnp.arange(hd // 2, dtype=F32) / hd)
        ang = inv_freq[:, None] * jnp.arange(seq).astype(F32)[None, :]
        cos_t, sin_t = jnp.cos(ang), jnp.sin(ang)

        hm_loc, hk_loc, hs_loc = norm_m(c1, x_loc, ln_params)
        at_loc, du_loc, dhm_loc = mlp_own(hm_loc, dy_loc, w_up, w_down)
        dctx_loc = dot(w_out, dy_loc, 1, 1).astype(BF)

        x_rem = after(x_rem, dhm_loc, dctx_loc, cos_t, sin_t, w_t)
        hm_rem, hk_rem, hs_rem = norm_m(c1, x_rem, ln_params)
        h_a, h_keep, h_send = norm_a(c1, x_loc, x_rem, ln_params)
        qkv_t = dot(w_t, h_a, 1, 1).astype(BF)

        at_rem, slope = mlp_pre(after(hm_rem, qkv_t), w_up)

        dy_rem = after(dy_rem, qkv_t, h_keep, slope)
        d_out, d_stay, uka, ukb, usa, usb, dhm_rem, dctx_rem = mlp_peer(
            dy_rem, dy_loc, (hk_loc, hs_loc, hk_rem, hs_rem), w_up, w_down, w_out, at_loc, at_rem, du_loc, slope)
        dq, ctx, g_wdown, u_send, u_keep = attention(
            qkv_t, dctx_loc, dctx_rem, cos_t, sin_t, (d_out, d_stay), (uka, ukb, usa, usb), hd)
        grad_x, sums, g_wqkv, g_wout, g_wup, g_wdown = emit(*tail(
            dq, ctx, h_keep, h_send, w_t, x_loc, x_rem, dhm_loc, dhm_rem, dy_loc, dy_rem, ln_params, u_keep, u_send, hd), g_wdown)
        grad_x = grad_x[None]
        g_wqkv = g_wqkv.reshape(heads, 3, hd, d // dp).transpose(3, 0, 1, 2)
        return grad_x, sums, g_wqkv, g_wout, g_wup, g_wdown

    return jax.shard_map(
        local_step,
        mesh=mesh,
        in_specs=(P("dp", "tp"), P("dp", "tp"), P(), P(None, "tp"), P("tp"), P(None, "tp"), P("tp")),
        out_specs=(P("dp", "tp"), P(), P("dp", "tp"), P(("tp", "dp")), P("dp", "tp"), P(("tp", "dp"))),
        check_vma=False,
    )
```

profile of v0, /device:TPU:0, one launch (start us, length us, event | category | flops | bytes accessed | tf_op | source)
XLA Modules:
  0.0 230.5 jit_solution(16013347016801560448)
XLA Ops:
  0.6 3.3 %collective-permute-start = (bf16[768,1024]{1,0:T(8,128)(2,1)}, bf16[768,1024]{1,0:T(8,128)(2,1)S(1)}, u32[]{:S(2)}, u32[]{:S(2)}) collective-permute-start(bf16[768,1024]{1,0:T(8,128)(2,1)} %bitcast.19), channel_id=1, source_target_pairs={{0,8},{8,0},{1,9},{9,1},{2,10},{10,2},{3,11},{11,3},{4,12},{12,4},... | collective-permute-start | bytes 4718600 | tf_op jit(solution)/shard_map/ppermute | solution.py:727
  3.9 0.1 collective-permute-start.1
  4.0 3.6 %convolution_convert_fusion.1.dol_ref = bf16[512,768]{1,0:T(8,128)(2,1)} fusion(bf16[512,1024]{1,0:T(8,128)(2,1)} %wo_ref.1, bf16[1,768,1024]{2,1,0:T(8,128)(2,1)} %param.8), kind=kOutput, calls=%fused_computation.2 | convolution fusion | flops 805699584 | bytes 3407872 | tf_op jit(solution)/shard_map/dot_general | solution.py:20
  7.6 4.3 %norm_m.2 = (bf16[768,1024]{1,0:T(8,128)(2,1)}, bf16[512,768]{1,0:T(8,128)(2,1)}, bf16[512,768]{1,0:T(8,128)(2,1)}) custom-call(s32[1]{0:T(128)} %bitcast.c_ref, bf16[768,1024]{1,0:T(8,128)(2,1)} %bitcast.20, f32[4,1024]{1,0:T(4,128)} %refs_11_.1), custom_call_target="tpu_custom_call" | custom-call | flops 3000000000 | bytes 4718592 | tf_op jit(solution)/shard_map/norm_m/pallas_call | solution.py:50
  11.9 1.5 multiply_sine_fusion
  13.4 19.1 %mlp_own.1 = (bf16[2048,768]{1,0:T(8,128)(2,1)}, bf16[4,768,512]{2,1,0:T(8,128)(2,1)}, bf16[768,1024]{1,0:T(8,128)(2,1)}) custom-call(bf16[768,1024]{1,0:T(8,128)(2,1)} %get-tuple-element.47.h_ref, bf16[768,1024]{1,0:T(8,128)(2,1)} %bitcast.24, bf16[1024,2048]{1,0:T(8,128)(2,1)} %wu_ref.5, bf16[2048,1024]{1,0:T(8,128)(2,1)} %wd_ref.3), custom_call_target="tpu_custom_call" | custom-call | flops 9663676416 | bytes 20971520 | tf_op jit(solution)/shard_map/mlp_own/pallas_call | solution.py:345
  32.5 6.9 %collective-permute-done.xr_ref.x_ref.refs_6_ = bf16[768,1024]{1,0:T(8,128)(2,1)S(1)} collective-permute-done((bf16[768,1024]{1,0:T(8,128)(2,1)}, bf16[768,1024]{1,0:T(8,128)(2,1)S(1)}, u32[]{:S(2)}, u32[]{:S(2)}) %collective-permute-start) | collective-permute-done | bytes 1572896 | tf_op jit(solution)/shard_map/ppermute | solution.py:727
  39.4 0.0 copy-start.1
  39.4 1.1 copy-done.1
  40.5 7.2 %norm_a.1 = (bf16[1536,1024]{1,0:T(8,128)(2,1)}, bf16[1536,512]{1,0:T(8,128)(2,1)}, bf16[1536,512]{1,0:T(8,128)(2,1)}) custom-call(s32[1]{0:T(128)} %bitcast.c_ref, bf16[768,1024]{1,0:T(8,128)(2,1)} %bitcast.21, bf16[768,1024]{1,0:T(8,128)(2,1)} %copy-done.1, f32[4,1024]{1,0:T(4,128)} %refs_11_.1), custom_call_target="tpu_custom_call" | custom-call | flops 6000000000 | bytes 9437184 | tf_op jit(solution)/shard_map/norm_a/pallas_call | solution.py:83
  47.8 0.0 copy-start
  47.8 4.5 %norm_m.3 = (bf16[768,1024]{1,0:T(8,128)(2,1)}, bf16[512,768]{1,0:T(8,128)(2,1)}, bf16[512,768]{1,0:T(8,128)(2,1)}) custom-call(s32[1]{0:T(128)} %bitcast.c_ref, bf16[768,1024]{1,0:T(8,128)(2,1)} %copy-done.1, f32[4,1024]{1,0:T(4,128)} %refs_11_.1), custom_call_target="tpu_custom_call" | custom-call | flops 3000000000 | bytes 4718592 | tf_op jit(solution)/shard_map/norm_m/pallas_call | solution.py:50
  52.3 0.0 copy-done
  52.3 8.6 %fusion.qkv_ref = bf16[1536,1536]{1,0:T(8,128)(2,1)} fusion(bf16[1536,1024]{1,0:T(8,128)(2,1)} %get-tuple-element.50, bf16[1536,1024]{1,0:T(8,128)(2,1)S(1)} %bitcast.18), kind=kOutput, calls=%fused_computation.1 | convolution fusion | flops 4834197504 | bytes 11010048 | tf_op jit(solution)/shard_map/dot_general | solution.py:20
  60.9 10.0 %mlp_pre.1 = (bf16[2048,768]{1,0:T(8,128)(2,1)}, f32[4,768,512]{2,1,0:T(8,128)}) custom-call(bf16[768,1024]{1,0:T(8,128)(2,1)} %get-tuple-element.53.h_ref, bf16[1024,2048]{1,0:T(8,128)(2,1)} %wu_ref.5), custom_call_target="tpu_custom_call" | custom-call | flops 3221225472 | bytes 16777216 | tf_op jit(solution)/shard_map/mlp_pre/pallas_call | solution.py:373
  70.9 1.4 collective-permute-done.1.dyr_ref.refs_10_
  72.4 36.3 %mlp_peer.1 = (f32[2,2,256,512]{3,2,1,0:T(8,128)}, f32[2,2,256,512]{3,2,1,0:T(8,128)}, f32[4,4,128,256]{3,2,1,0:T(8,128)}, f32[4,4,128,256]{3,2,1,0:T(8,128)}, f...) custom-call(bf16[768,1024]{1,0:T(8,128)(2,1)} %collective-permute-do, ...), custom_call_target="tpu_custom_call" | custom-call | flops 22548578304 | bytes 41943040 | tf_op jit(solution)/shard_map/mlp_peer/pallas_call | solution.py:461
  108.6 64.3 %attn.1 = (bf16[1536,1536]{1,0:T(8,128)(2,1)}, bf16[512,1536]{1,0:T(8,128)(2,1)}, f32[256,1024]{1,0:T(8,128)}, f32[2,4,128,256]{3,2,1,0:T(8,128)}, f32[2,4,128,256]{3,2,1,0:T(8,128)}) custom-call(bf16[1536,1536]{1,0:T(8,128)(2,1)} %fusion.qkv_ref, bf16[512,768]{1,0:T(8,128)(2,1)} %convolution_convert_fusion.1.dol_ref, ...), custom_call_target="tpu_custom_call" | custom-call | flops 48000000000 | bytes 8388608 | tf_op jit(solution)/shard_map/attn/pallas_call | solution.py:292
  172.9 53.7 %tail.1 = (bf16[768,1024]{1,0:T(8,128)(2,1)}, f32[4,1024]{1,0:T(4,128)}, f32[1536,128]{1,0:T(8,128)}, f32[64,1024]{1,0:T(8,128)}, f32[128,2048]{1,0:T(8,128)}) custom-call(bf16[1536,1536]{1,0:T(8,128)(2,1)} %get-tuple-element.70.refs_0_, bf16[512,1536]{1,0:T(8,128)(2,1)} %get-tuple-element.71.refs_1_, bf16[1536,512]{1,0:T(8,128)(2,1)} %get-tuple-element.51.refs_2_, ...), custom_call_target="tpu_custom_call" | custom-call | flops 40000000000 | bytes 41943040 | tf_op jit(solution)/shard_map/tail/pallas_call | solution.py:681
  226.6 3.7 %emit.1 = (bf16[768,1024]{1,0:T(8,128)(2,1)}, f32[4,1024]{1,0:T(4,128)}, f32[1536,128]{1,0:T(8,128)}, f32[64,1024]{1,0:T(8,128)}, f32[128,2048]{1,0:T(8,128)}, /*index=5*/f32[256,1024]{1,0:T(8,128)}) custom-call(bf16[768,1024]{1,0:T(8,128)(2,1)} %get-tuple-element.76.refs_0_, f32[4,1024]{1,0:T(4,128)} %get-tuple-element.77.refs_1_, ...), custom_call_target="tpu_custom_call" | custom-call | flops 1000000 | bytes 10485760 | tf_op jit(solution)/shard_map/emit/pallas_call | solution.py:709
  (2 shorter events, 0.0 us)
Async XLA Ops:
  0.6 38.8 %collective-permute-start = (bf16[768,1024]{1,0:T(8,128)(2,1)}, bf16[768,1024]{1,0:T(8,128)(2,1)S(1)}, u32[]{:S(2)}, u32[]{:S(2)}) collective-permute-start(bf16[768,1024]{1,0:T(8,128)(2,1)} %bitcast.19), channel_id=1, source_target_pairs={{0,8},{8,0},{1,9},{9,1},{2,10},{10,2},{3,11},{11,3},{4,12},{12,4},... | collective-permute-start | bytes 4718600 | tf_op jit(solution)/shard_map/ppermute | solution.py:727
  3.9 68.4 %collective-permute-start.1 = (bf16[768,1024]{1,0:T(8,128)(2,1)}, bf16[768,1024]{1,0:T(8,128)(2,1)}, u32[]{:S(2)}, u32[]{:S(2)}) collective-permute-start(bf16[768,1024]{1,0:T(8,128)(2,1)} %bitcast.23), channel_id=1, source_target_pairs={{0,8},{8,0},{1,9},{9,1},{2,10},{10,2},{3,11},{11,3},{4,12},{12,4},... | collective-permute-start | bytes 4718600 | tf_op jit(solution)/shard_map/ppermute | solution.py:727
  39.4 1.1 copy-start.1
  47.8 4.5 %copy-start = (bf16[1024,8,3,64]{0,3,2,1:T(8,128)(2,1)S(1)}, bf16[1024,8,3,64]{0,3,2,1:T(8,128)(2,1)}, u32[]{:S(2)}) copy-start(bf16[1024,8,3,64]{0,3,2,1:T(8,128)(2,1)} %param.10) | copy-start | bytes 9437188
where the time goes:
time: 231 us; the launch traced here: 230 us
  Pallas kernels  203 us (88%)
  matrix products  12.3 us (5%)
  waiting for transfers between devices  8.3 us (4%)
  starting transfers between devices  3.37 us (1%)
    pallas_call x1, Pallas kernels, attention(): pl.pallas_call(functools.partial(attn_kernel, bq=bq, hd=hd), grid=(heads,...  64.3 us
    pallas_call x1, Pallas kernels, tail(): pl.pallas_call(functools.partial(tail_kernel, bt=bt, hd=hd), in_specs=[pl...  53.7 us
    pallas_call x1, Pallas kernels, mlp_peer(): pl.pallas_call(functools.partial(mlp_peer_kernel, tc=tc), grid=(n,), in_s...  36.3 us
    pallas_call x1, Pallas kernels, mlp_own(): pl.pallas_call(functools.partial(mlp_own_kernel, tc=tc), grid=(n,), in_sp...  19.1 us
    dot_general x2, matrix products, dot(): lax.dot_general(a, b, (((ca,), (cb,)), ((), ())), preferred_element_type=...  12.3 us
    pallas_call x1, Pallas kernels, mlp_pre(): pl.pallas_call(functools.partial(mlp_pre_kernel, tc=tc), grid=(n,), in_sp...  10 us
    pallas_call x2, Pallas kernels, norm_m(): pl.pallas_call(norm_m_kernel, grid_spec=pltpu.PrefetchScalarGridSpec(num_...  8.81 us
    ppermute x2, waiting for transfers between devices, swap_tp(): return lax.ppermute(v, 'tp', [(i, i ^ 1) for i in range(tp)])  8.3 us
  transfers between devices with their start and end apart: 2, of which 2 were waited for; matrix products, arithmetic and copies ran while one was open for 6% of the time, Pallas kernels for 20%

commit v1 on v0

--- a/solution.py
+++ b/solution.py
@@ -130,8 +130,8 @@
 def attn_kernel(qkv_ref, dol_ref, dor_ref, cos_ref, sin_ref,
                 d_out, d_stay, uka, ukb, usa, usb,
                 dqkv_ref, ctx_ref, gd_ref, us_ref, uk_ref,
-                dk_ref, dv_ref, d_keep, u_keep, u_got, d1_got, u1_send, u1_got, d2_send, d2_got,
-                load_sem, send_sem, recv_sem, *, bq, hd):
+                dk_ref, dv_ref, d_keep, u_keep, u_got, d1_got, u1_send, u1_got, d2_send, d2_got, us_buf, uk_buf,
+                load_sem, store_sem, send_sem, recv_sem, *, bq, hd):
     way, t, _, xx, yy = partners()
     step = pl.program_id(0)
     last = pl.num_programs(0) - 1
@@ -145,6 +145,7 @@
     second_d = [remote(4 + k, d2_send.at[k], d2_got.at[k], WAYS[k][1]) for k in range(2)]
     first_u = [remote(6 + k, u1_send.at[k], u1_got.at[k], WAYS[k][0]) for k in range(2)]
     load_d = pltpu.make_async_copy(d_stay, d_keep, load_sem.at[0])
+    stores = [pltpu.make_async_copy(v, o, store_sem.at[k]) for k, (v, o) in enumerate(((us_buf, us_ref), (uk_buf, uk_ref)))]
     load_u = [pltpu.make_async_copy(src, u_keep.at[k], load_sem.at[2 + k]) for k, src in enumerate((uka, ukb))]
 
     leave = [lambda i: 2 * i + 1 - xx, lambda i: 2 * (1 - yy) + i]
@@ -193,15 +194,19 @@
 
             def add(r):
                 for j in range(u_keep.shape[1]):
-                    us_ref[k, j, r, :] = u_keep[k, j, stay[k](1 - m), r, :] + u1_got[k, 1 - m, j, r, :]
-                    uk_ref[k, j, r, :] = u_keep[k, j, stay[k](m), r, :] + u1_got[k, m, j, r, :]
+                    us_buf[k, j, r, :] = u_keep[k, j, stay[k](1 - m), r, :] + u1_got[k, 1 - m, j, r, :]
+                    uk_buf[k, j, r, :] = u_keep[k, j, stay[k](m), r, :] + u1_got[k, m, j, r, :]
 
             by_rows(u_keep.shape[3], 16, add)
+        for v in stores:
+            v.start()
 
     attn_head(t, qkv_ref, dol_ref, dor_ref, cos_ref, sin_ref, dqkv_ref, ctx_ref, dk_ref, dv_ref, bq, hd)
 
     @pl.when(step == last)
     def _():
+        for v in stores:
+            v.wait()
         w = d_keep.shape[3]
         for k in range(2):
             second_d[k].wait()
@@ -293,12 +298,12 @@
         functools.partial(attn_kernel, bq=bq, hd=hd),
         grid=(heads,),
         in_specs=[row(3 * hd, seq), row(hd, part), row(hd, part), const, const] + [hbm] * 6,
-        out_specs=[row(3 * hd, seq), row(hd, seq), whole(*gd_shape), whole(2, *ured), whole(2, *ured)],
+        out_specs=[row(3 * hd, seq), row(hd, seq), whole(*gd_shape), hbm, hbm],
         out_shape=[sds((rows, seq), BF), sds((heads * hd, seq), BF), sds(gd_shape, F32), sds((2,) + ured, F32), sds((2,) + ured, F32)],
         scratch_shapes=[
             f(seq, hd), f(seq, hd), f(*dsh), f(2, *ush), f(2, *ush),
-            f(*dsh), f(2, 2, *ured), f(2, 2, *ured), f(2, *dred), f(2, *dred),
-            pltpu.SemaphoreType.DMA((4,)), pltpu.SemaphoreType.DMA((10,)), pltpu.SemaphoreType.DMA((10,)),
+            f(*dsh), f(2, 2, *ured), f(2, 2, *ured), f(2, *dred), f(2, *dred), f(2, *ured), f(2, *ured),
+            pltpu.SemaphoreType.DMA((4,)), pltpu.SemaphoreType.DMA((2,)), pltpu.SemaphoreType.DMA((10,)), pltpu.SemaphoreType.DMA((10,)),
         ],
         compiler_params=pltpu.CompilerParams(vmem_limit_bytes=VMEM_LIMIT, collective_id=1, has_side_effects=True),
         cost_estimate=cost(heads * 6e9, heads << 20, seq * seq * heads // 2),
@@ -382,9 +387,10 @@
     )(h, w_up)
 
 
-def mlp_peer_kernel(dyr_ref, dyl_ref, hkl_ref, hsl_ref, hkr_ref, hsr_ref, wu_ref, wd_ref, wo_ref, at_ref, atr_ref, dul_ref, gp_ref,
+def mlp_peer_kernel(dyr_ref, dyl_hbm, hkl_hbm, hsl_hbm, hkr_hbm, hsr_hbm, wu_ref, wd_ref, wo_ref, at_ref, atr_ref, dul_ref, gp_ref,
                     d_out, d_stay, uka_ref, ukb_ref, usa_ref, usb_ref, dh_ref, dctx_ref,
-                    acc_ref, du_ref, d_keep, d_send, d_got, send_sem, recv_sem, *, tc):
+                    acc_ref, du_ref, d_keep, d_send, d_got, dyl_ref, hkl_ref, hsl_ref, hkr_ref, hsr_ref,
+                    send_sem, recv_sem, load_sem, store_sem, *, tc):
     way, _, c, xx, yy = partners()
     step = pl.program_id(0)
     last = pl.num_programs(0) - 1
@@ -399,15 +405,28 @@
 
     def combine(i):
         remote(i).wait()
+        for k in range(2):
+            def add(r):
+                d_keep[i, k, r, :] += d_got[i, k, r, :]
+
+            by_rows(m, 32, add)
+        store(i, lambda v: v.start())
+
+    def store(i, f):
         y, x = i // 2, i % 2
         for k, at, go in ((0, y, x != xx), (1, x, y != yy)):
             for ref, cond in ((d_out, go), (d_stay, jnp.logical_not(go))):
                 @pl.when(cond)
                 def _():
-                    def add(r):
-                        ref[k, at, r, :] = d_keep[i, k, r, :] + d_got[i, k, r, :]
-
-                    by_rows(m, 32, add)
+                    f(pltpu.make_async_copy(d_keep.at[i, k], ref.at[k, at], store_sem.at[i, k]))
+
+    late = [pltpu.make_async_copy(src, dst, load_sem.at[k]) for k, (src, dst) in enumerate((
+        (dyl_hbm, dyl_ref), (hkl_hbm, hkl_ref), (hsl_hbm, hsl_ref), (hkr_hbm, hkr_ref), (hsr_hbm, hsr_ref)))]
+
+    @pl.when(step == 0)
+    def _():
+        for v in late:
+            v.start()
 
     pl.when(step == 0)(lambda: meet(way, "c"))
     dctx_ref[...] = dot(wo_ref[...], dyr_ref[...], 1, 1).astype(BF)
@@ -422,6 +441,12 @@
         du = (dg * gp_ref[0, rows, :]).astype(BF)
         du_ref[rows, :] = du
         acc_ref[rows, :] += dot(du, wu, 1, 1)
+
+    @pl.when(step == 0)
+    def _():
+        for v in late:
+            v.wait()
+
     for side, ref in ((1 - c, d_send), (c, d_keep)):
         block = pl.ds(pl.multiple_of(side * m, 128), m)
         g = dot(at_ref[block, :], dyl_ref[...], 1, 0) + dot(atr_ref[block, :], dyr_ref[...], 1, 0)
@@ -443,6 +468,8 @@
     def _():
         combine(step)
         dh_ref[...] = acc_ref[...].astype(BF)
+        for i in range(4):
+            store(i, lambda v: v.wait())
 
 
 def mlp_peer(dy_rem, dy_loc, hts, w_up, w_down, w_out, at, at_rem, du, slope, n=4, tc=256):
@@ -453,7 +480,7 @@
     full = lambda r, w: pl.BlockSpec((r, w), lambda i: (0, 0))
     rows = lambda r, w: pl.BlockSpec((r, w), lambda i: (i, 0))
     dshape = (2, 2, fb // 2, d // 2)
-    dspec = pl.BlockSpec(dshape, lambda i: (0, 0, 0, 0))
+    hbm = pl.BlockSpec(memory_space=pl.ANY)
     uspec = pl.BlockSpec((1, 4, d // 8, fb // 2), lambda i: (i, 0, 0, 0))
     act = pl.BlockSpec((1, seq, fb), lambda i: (i, 0, 0))
     sds = jax.ShapeDtypeStruct
@@ -461,12 +488,14 @@
     return pl.pallas_call(
         functools.partial(mlp_peer_kernel, tc=tc),
         grid=(n,),
-        in_specs=[full(seq, d)] * 2 + [full(d // 2, seq)] * 4 + [
+        in_specs=[full(seq, d)] + [hbm] * 5 + [
             pl.BlockSpec((d, fb), lambda i: (0, i)), rows(fb, d), rows(ctx // n, d), rows(fb, seq), rows(fb, seq), act, act],
-        out_specs=[dspec] * 2 + [uspec] * 4 + [full(seq, d), rows(ctx // n, seq)],
+        out_specs=[hbm] * 2 + [uspec] * 4 + [full(seq, d), rows(ctx // n, seq)],
         out_shape=[sds(dshape, F32)] * 2 + [sds((n, 4, d // 8, fb // 2), F32)] * 4 + [sds((seq, d), BF), sds((ctx, seq), BF)],
         scratch_shapes=[pltpu.VMEM((seq, d), F32), pltpu.VMEM((seq, fb), BF), slots, slots, slots,
-                        pltpu.SemaphoreType.DMA((n,)), pltpu.SemaphoreType.DMA((n,))],
+                        pltpu.VMEM((seq, d), BF)] + [pltpu.VMEM((d // 2, seq), BF)] * 4 + [
+                        pltpu.SemaphoreType.DMA((n,)), pltpu.SemaphoreType.DMA((n,)),
+                        pltpu.SemaphoreType.DMA((5,)), pltpu.SemaphoreType.DMA((n, 2))],
         compiler_params=pltpu.CompilerParams(vmem_limit_bytes=63 * 1024 * 1024, collective_id=2, has_side_effects=True),
         cost_estimate=cost(14 * seq * d * ff, 40 << 20),
         name="mlp_peer",

time: 231 us -> 229 us (level)
  no operation moved by 1% of the time
where the time goes in v1:
time: 229 us
  Pallas kernels  201 us (88%)
  matrix products  12.3 us (5%)
  waiting for transfers between devices  8.3 us (4%)
  starting transfers between devices  3.37 us (1%)
    pallas_call x1, Pallas kernels, attention(): pl.pallas_call(functools.partial(attn_kernel, bq=bq, hd=hd), grid=(heads,...  63.6 us
    pallas_call x1, Pallas kernels, tail(): pl.pallas_call(functools.partial(tail_kernel, bt=bt, hd=hd), in_specs=[pl...  53.7 us
    pallas_call x1, Pallas kernels, mlp_peer(): pl.pallas_call(functools.partial(mlp_peer_kernel, tc=tc), grid=(n,), in_s...  35.3 us
    pallas_call x1, Pallas kernels, mlp_own(): pl.pallas_call(functools.partial(mlp_own_kernel, tc=tc), grid=(n,), in_sp...  19.1 us
    dot_general x2, matrix products, dot(): lax.dot_general(a, b, (((ca,), (cb,)), ((), ())), preferred_element_type=...  12.3 us
    pallas_call x1, Pallas kernels, mlp_pre(): pl.pallas_call(functools.partial(mlp_pre_kernel, tc=tc), grid=(n,), in_sp...  10 us
    pallas_call x2, Pallas kernels, norm_m(): pl.pallas_call(norm_m_kernel, grid_spec=pltpu.PrefetchScalarGridSpec(num_...  8.81 us
    ppermute x2, waiting for transfers between devices, swap_tp(): return lax.ppermute(v, 'tp', [(i, i ^ 1) for i in range(tp)])  8.3 us
  transfers between devices with their start and end apart: 2, of which 2 were waited for; matrix products, arithmetic and copies ran while one was open for 6% of the time, Pallas kernels for 20%

profile of v1, /device:TPU:0, one launch (start us, length us, event | category | flops | bytes accessed | tf_op | source)
XLA Modules:
  0.0 228.9 jit_solution(2922573176780474591)
XLA Ops:
  0.6 3.3 %collective-permute-start = (bf16[768,1024]{1,0:T(8,128)(2,1)}, bf16[768,1024]{1,0:T(8,128)(2,1)S(1)}, u32[]{:S(2)}, u32[]{:S(2)}) collective-permute-start(bf16[768,1024]{1,0:T(8,128)(2,1)} %bitcast.19), channel_id=1, source_target_pairs={{0,8},{8,0},{1,9},{9,1},{2,10},{10,2},{3,11},{11,3},{4,12},{12,4},... | collective-permute-start | bytes 4718600 | tf_op jit(solution)/shard_map/ppermute | solution.py:756
  3.9 0.1 collective-permute-start.1
  4.0 3.6 %convolution_convert_fusion.1.dol_ref = bf16[512,768]{1,0:T(8,128)(2,1)} fusion(bf16[512,1024]{1,0:T(8,128)(2,1)} %wo_ref.1, bf16[1,768,1024]{2,1,0:T(8,128)(2,1)} %param.8), kind=kOutput, calls=%fused_computation.2 | convolution fusion | flops 805699584 | bytes 3407872 | tf_op jit(solution)/shard_map/dot_general | solution.py:20
  7.6 4.3 %norm_m.2 = (bf16[768,1024]{1,0:T(8,128)(2,1)}, bf16[512,768]{1,0:T(8,128)(2,1)}, bf16[512,768]{1,0:T(8,128)(2,1)}) custom-call(s32[1]{0:T(128)} %bitcast.c_ref, bf16[768,1024]{1,0:T(8,128)(2,1)} %bitcast.20, f32[4,1024]{1,0:T(4,128)} %refs_11_.1), custom_call_target="tpu_custom_call" | custom-call | flops 3000000000 | bytes 4718592 | tf_op jit(solution)/shard_map/norm_m/pallas_call | solution.py:50
  11.9 1.5 multiply_sine_fusion
  13.4 19.1 %mlp_own.1 = (bf16[2048,768]{1,0:T(8,128)(2,1)}, bf16[4,768,512]{2,1,0:T(8,128)(2,1)}, bf16[768,1024]{1,0:T(8,128)(2,1)}) custom-call(bf16[768,1024]{1,0:T(8,128)(2,1)} %get-tuple-element.47.h_ref, bf16[768,1024]{1,0:T(8,128)(2,1)} %bitcast.24, bf16[1024,2048]{1,0:T(8,128)(2,1)} %wu_ref.5, bf16[2048,1024]{1,0:T(8,128)(2,1)} %wd_ref.3), custom_call_target="tpu_custom_call" | custom-call | flops 9663676416 | bytes 20971520 | tf_op jit(solution)/shard_map/mlp_own/pallas_call | solution.py:350
  32.5 6.9 %collective-permute-done.xr_ref.x_ref.refs_6_ = bf16[768,1024]{1,0:T(8,128)(2,1)S(1)} collective-permute-done((bf16[768,1024]{1,0:T(8,128)(2,1)}, bf16[768,1024]{1,0:T(8,128)(2,1)S(1)}, u32[]{:S(2)}, u32[]{:S(2)}) %collective-permute-start) | collective-permute-done | bytes 1572896 | tf_op jit(solution)/shard_map/ppermute | solution.py:756
  39.4 0.0 copy-start.1
  39.4 1.1 copy-done.1
  40.5 7.2 %norm_a.1 = (bf16[1536,1024]{1,0:T(8,128)(2,1)}, bf16[1536,512]{1,0:T(8,128)(2,1)}, bf16[1536,512]{1,0:T(8,128)(2,1)}) custom-call(s32[1]{0:T(128)} %bitcast.c_ref, bf16[768,1024]{1,0:T(8,128)(2,1)} %bitcast.21, bf16[768,1024]{1,0:T(8,128)(2,1)} %copy-done.1, f32[4,1024]{1,0:T(4,128)} %refs_11_.1), custom_call_target="tpu_custom_call" | custom-call | flops 6000000000 | bytes 9437184 | tf_op jit(solution)/shard_map/norm_a/pallas_call | solution.py:83
  47.8 0.0 copy-start
  47.8 4.5 %norm_m.3 = (bf16[768,1024]{1,0:T(8,128)(2,1)}, bf16[512,768]{1,0:T(8,128)(2,1)}, bf16[512,768]{1,0:T(8,128)(2,1)}) custom-call(s32[1]{0:T(128)} %bitcast.c_ref, bf16[768,1024]{1,0:T(8,128)(2,1)} %copy-done.1, f32[4,1024]{1,0:T(4,128)} %refs_11_.1), custom_call_target="tpu_custom_call" | custom-call | flops 3000000000 | bytes 4718592 | tf_op jit(solution)/shard_map/norm_m/pallas_call | solution.py:50
  52.3 0.0 copy-done
  52.3 8.6 %fusion.qkv_ref = bf16[1536,1536]{1,0:T(8,128)(2,1)} fusion(bf16[1536,1024]{1,0:T(8,128)(2,1)} %get-tuple-element.50, bf16[1536,1024]{1,0:T(8,128)(2,1)S(1)} %bitcast.18), kind=kOutput, calls=%fused_computation.1 | convolution fusion | flops 4834197504 | bytes 11010048 | tf_op jit(solution)/shard_map/dot_general | solution.py:20
  60.9 10.0 %mlp_pre.1 = (bf16[2048,768]{1,0:T(8,128)(2,1)}, f32[4,768,512]{2,1,0:T(8,128)}) custom-call(bf16[768,1024]{1,0:T(8,128)(2,1)} %get-tuple-element.53.h_ref, bf16[1024,2048]{1,0:T(8,128)(2,1)} %wu_ref.5), custom_call_target="tpu_custom_call" | custom-call | flops 3221225472 | bytes 16777216 | tf_op jit(solution)/shard_map/mlp_pre/pallas_call | solution.py:378
  70.9 1.4 collective-permute-done.1.dyr_ref.refs_10_
  72.4 35.3 %mlp_peer.1 = (f32[2,2,256,512]{3,2,1,0:T(8,128)}, f32[2,2,256,512]{3,2,1,0:T(8,128)}, f32[4,4,128,256]{3,2,1,0:T(8,128)}, f32[4,4,128,256]{3,2,1,0:T(8,128)}, f...) custom-call(bf16[768,1024]{1,0:T(8,128)(2,1)} %collective-permute-do, ...), custom_call_target="tpu_custom_call" | custom-call | flops 22548578304 | bytes 41943040 | tf_op jit(solution)/shard_map/mlp_peer/pallas_call | solution.py:488
  107.7 63.6 %attn.1 = (bf16[1536,1536]{1,0:T(8,128)(2,1)}, bf16[512,1536]{1,0:T(8,128)(2,1)}, f32[256,1024]{1,0:T(8,128)}, f32[2,4,128,256]{3,2,1,0:T(8,128)}, f32[2,4,128,256]{3,2,1,0:T(8,128)}) custom-call(bf16[1536,1536]{1,0:T(8,128)(2,1)} %fusion.qkv_ref, bf16[512,768]{1,0:T(8,128)(2,1)} %convolution_convert_fusion.1.dol_ref, ...), custom_call_target="tpu_custom_call" | custom-call | flops 48000000000 | bytes 8388608 | tf_op jit(solution)/shard_map/attn/pallas_call | solution.py:297
  171.3 53.7 %tail.1 = (bf16[768,1024]{1,0:T(8,128)(2,1)}, f32[4,1024]{1,0:T(4,128)}, f32[1536,128]{1,0:T(8,128)}, f32[64,1024]{1,0:T(8,128)}, f32[128,2048]{1,0:T(8,128)}) custom-call(bf16[1536,1536]{1,0:T(8,128)(2,1)} %get-tuple-element.70.refs_0_, bf16[512,1536]{1,0:T(8,128)(2,1)} %get-tuple-element.71.refs_1_, bf16[1536,512]{1,0:T(8,128)(2,1)} %get-tuple-element.51.refs_2_, ...), custom_call_target="tpu_custom_call" | custom-call | flops 40000000000 | bytes 41943040 | tf_op jit(solution)/shard_map/tail/pallas_call | solution.py:710
  225.0 3.7 %emit.1 = (bf16[768,1024]{1,0:T(8,128)(2,1)}, f32[4,1024]{1,0:T(4,128)}, f32[1536,128]{1,0:T(8,128)}, f32[64,1024]{1,0:T(8,128)}, f32[128,2048]{1,0:T(8,128)}, /*index=5*/f32[256,1024]{1,0:T(8,128)}) custom-call(bf16[768,1024]{1,0:T(8,128)(2,1)} %get-tuple-element.76.refs_0_, f32[4,1024]{1,0:T(4,128)} %get-tuple-element.77.refs_1_, ...), custom_call_target="tpu_custom_call" | custom-call | flops 1000000 | bytes 10485760 | tf_op jit(solution)/shard_map/emit/pallas_call | solution.py:738
  (2 shorter events, 0.0 us)
Async XLA Ops:
  0.6 38.8 %collective-permute-start = (bf16[768,1024]{1,0:T(8,128)(2,1)}, bf16[768,1024]{1,0:T(8,128)(2,1)S(1)}, u32[]{:S(2)}, u32[]{:S(2)}) collective-permute-start(bf16[768,1024]{1,0:T(8,128)(2,1)} %bitcast.19), channel_id=1, source_target_pairs={{0,8},{8,0},{1,9},{9,1},{2,10},{10,2},{3,11},{11,3},{4,12},{12,4},... | collective-permute-start | bytes 4718600 | tf_op jit(solution)/shard_map/ppermute | solution.py:756
  3.9 68.4 %collective-permute-start.1 = (bf16[768,1024]{1,0:T(8,128)(2,1)}, bf16[768,1024]{1,0:T(8,128)(2,1)}, u32[]{:S(2)}, u32[]{:S(2)}) collective-permute-start(bf16[768,1024]{1,0:T(8,128)(2,1)} %bitcast.23), channel_id=1, source_target_pairs={{0,8},{8,0},{1,9},{9,1},{2,10},{10,2},{3,11},{11,3},{4,12},{12,4},... | collective-permute-start | bytes 4718600 | tf_op jit(solution)/shard_map/ppermute | solution.py:756
  39.4 1.1 copy-start.1
  47.8 4.5 %copy-start = (bf16[1024,8,3,64]{0,3,2,1:T(8,128)(2,1)S(1)}, bf16[1024,8,3,64]{0,3,2,1:T(8,128)(2,1)}, u32[]{:S(2)}) copy-start(bf16[1024,8,3,64]{0,3,2,1:T(8,128)(2,1)} %param.10) | copy-start | bytes 9437188

commit v2 on v1

--- a/solution.py
+++ b/solution.py
@@ -505,11 +505,11 @@
 def tail_kernel(*refs, bt, hd):
     n_in = 13
     hbm, us_ref, refs = refs[:n_in], refs[n_in], refs[n_in + 1:]
-    (gx_ref, sums_ref, gq_ref, gw_ref, gu_ref), refs = refs[:5], refs[5:]
+    (gx_out, sums_ref, gq_ref, gw_ref, gu_out), refs = refs[:5], refs[5:]
     vm, refs = refs[:n_in], refs[n_in:]
     (z_send, z_recv, sum_src, sum_got, q_keep, q_send, q_recv, w_keep, w_send, w_recv,
-     q1_send, q1_recv, w1_send, w1_recv, q2_send, q2_recv, w2_send, w2_recv, u2_recv,
-     in_sem, send_sem, recv_sem) = refs
+     q1_send, q1_recv, w1_send, w1_recv, q2_send, q2_recv, w2_send, w2_recv, u2_recv, gx_ref, gu_ref,
+     out_sem, in_sem, send_sem, recv_sem) = refs
     dq, ctx, hk, hs, wt, xl, xr, dhl, dhr, dyl, dyr, ln, uk = vm
     way_to, t, c, xx, yy = partners()
     part = xl.shape[0]
@@ -638,6 +638,8 @@
         gx_ref[pl.ds(b * bt, bt), :] = dxh
         sum_src[0] += s
 
+    stores = []
+
     def grad_x(b):
         zs[b].wait()
         rows = pl.ds(b * bt, bt)
@@ -645,6 +647,8 @@
         xh, rstd = normalized(xl[rows, :].astype(F32))
         dx = rstd * (dxh - jnp.mean(dxh, -1, keepdims=True) - xh * jnp.mean(dxh * xh, -1, keepdims=True))
         gx_ref[rows, :] = (dyl[rows, :].astype(F32) + dx).astype(BF)
+        stores.append(pltpu.make_async_copy(gx_ref.at[rows], gx_out.at[rows], out_sem.at[b]))
+        stores[-1].start()
 
     own_block(0)
     q_second(2)
@@ -667,6 +671,8 @@
         us[k].wait()
         for j in range(blocks):
             gu_ref[:, (2 * j + k) * m:(2 * j + k + 1) * m] = uk[k, j] + u2_recv[k, j]
+    stores.append(pltpu.make_async_copy(gu_ref, gu_out, out_sem.at[part // bt]))
+    stores[-1].start()
     m = gw_ref.shape[1] // 2
     w2 = []
     for k in range(2):
@@ -687,6 +693,8 @@
     sums[-1].wait()
     sums_ref[...] = sum_src[3] + sum_got[3]
     grad_x(2)
+    for v in stores:
+        v.wait()
 
 
 def tail(dq, ctx, h_keep, h_send, w_t, x_loc, x_rem, dhm_loc, dhm_rem, dy_loc, dy_rem, ln, u_keep, u_send, hd, bt=256):
@@ -695,6 +703,7 @@
     rows = dq.shape[0] // 4
     nb = part // bt
     cols = d // 8
+    u_cols = u_keep.shape[0] * u_keep.shape[1] * u_keep.shape[3]
     f = lambda *shape: pltpu.VMEM(shape, F32)
     sds = jax.ShapeDtypeStruct
     scratch = [pltpu.VMEM(v.shape, v.dtype) for v in ins] + [
@@ -702,15 +711,15 @@
         f(4, 4, rows, cols), f(4, 4, rows, cols), f(4, 4, rows, cols),
         f(2, 4, hd, d // 2), f(2, 4, hd, d // 2), f(2, 4, hd, d // 2),
         f(4, 2, rows, cols), f(4, 2, rows, cols), f(2, 2, hd, d // 2), f(2, 2, hd, d // 2),
-        f(4, rows, cols), f(4, rows, cols), f(2, hd, d // 2), f(2, hd, d // 2), f(*u_send.shape),
+        f(4, rows, cols), f(4, rows, cols), f(2, hd, d // 2), f(2, hd, d // 2), f(*u_send.shape), pltpu.VMEM((part, d), BF), f(u_keep.shape[2], u_cols),
+        pltpu.SemaphoreType.DMA((nb + 1,)),
         pltpu.SemaphoreType.DMA((len(ins),)), pltpu.SemaphoreType.DMA((32,)), pltpu.SemaphoreType.DMA((32,)),
     ]
     vm = pl.BlockSpec(memory_space=pltpu.VMEM)
-    u_cols = u_keep.shape[0] * u_keep.shape[1] * u_keep.shape[3]
     return pl.pallas_call(
         functools.partial(tail_kernel, bt=bt, hd=hd),
         in_specs=[pl.BlockSpec(memory_space=pl.ANY)] * (len(ins) + 1),
-        out_specs=[vm] * 5,
+        out_specs=[pl.BlockSpec(memory_space=pl.ANY), vm, vm, vm, pl.BlockSpec(memory_space=pl.ANY)],
         out_shape=[sds((part, d), BF), sds((4, d), F32), sds((4 * rows, cols), F32), sds((hd, d), F32), sds((u_keep.shape[2], u_cols), F32)],
         scratch_shapes=scratch,
         compiler_params=pltpu.CompilerParams(vmem_limit_bytes=VMEM_LIMIT, collective_id=0, has_side_effects=True),

time: 229 us -> 230 us (level)
  no operation moved by 1% of the time
where the time goes in v2:
time: 230 us
  Pallas kernels  202 us (88%)
  matrix products  12.3 us (5%)
  waiting for transfers between devices  8.3 us (4%)
  starting transfers between devices  3.37 us (1%)
    pallas_call x1, Pallas kernels, attention(): pl.pallas_call(functools.partial(attn_kernel, bq=bq, hd=hd), grid=(heads,...  63.6 us
    pallas_call x1, Pallas kernels, tail(): pl.pallas_call(functools.partial(tail_kernel, bt=bt, hd=hd), in_specs=[pl...  54.3 us
    pallas_call x1, Pallas kernels, mlp_peer(): pl.pallas_call(functools.partial(mlp_peer_kernel, tc=tc), grid=(n,), in_s...  35.3 us
    pallas_call x1, Pallas kernels, mlp_own(): pl.pallas_call(functools.partial(mlp_own_kernel, tc=tc), grid=(n,), in_sp...  19.1 us
    dot_general x2, matrix products, dot(): lax.dot_general(a, b, (((ca,), (cb,)), ((), ())), preferred_element_type=...  12.3 us
    pallas_call x1, Pallas kernels, mlp_pre(): pl.pallas_call(functools.partial(mlp_pre_kernel, tc=tc), grid=(n,), in_sp...  10 us
    pallas_call x2, Pallas kernels, norm_m(): pl.pallas_call(norm_m_kernel, grid_spec=pltpu.PrefetchScalarGridSpec(num_...  8.81 us
    ppermute x2, waiting for transfers between devices, swap_tp(): return lax.ppermute(v, 'tp', [(i, i ^ 1) for i in range(tp)])  8.3 us
  transfers between devices with their start and end apart: 2, of which 2 were waited for; matrix products, arithmetic and copies ran while one was open for 6% of the time, Pallas kernels for 20%

profile of v2, /device:TPU:0, one launch (start us, length us, event | category | flops | bytes accessed | tf_op | source)
XLA Modules:
  0.0 229.5 jit_solution(920971441731453524)
XLA Ops:
  0.6 3.3 %collective-permute-start = (bf16[768,1024]{1,0:T(8,128)(2,1)}, bf16[768,1024]{1,0:T(8,128)(2,1)S(1)}, u32[]{:S(2)}, u32[]{:S(2)}) collective-permute-start(bf16[768,1024]{1,0:T(8,128)(2,1)} %bitcast.19), channel_id=1, source_target_pairs={{0,8},{8,0},{1,9},{9,1},{2,10},{10,2},{3,11},{11,3},{4,12},{12,4},... | collective-permute-start | bytes 4718600 | tf_op jit(solution)/shard_map/ppermute | solution.py:765
  3.9 0.1 collective-permute-start.1
  4.0 3.6 %convolution_convert_fusion.1.dol_ref = bf16[512,768]{1,0:T(8,128)(2,1)} fusion(bf16[512,1024]{1,0:T(8,128)(2,1)} %wo_ref.1, bf16[1,768,1024]{2,1,0:T(8,128)(2,1)} %param.8), kind=kOutput, calls=%fused_computation.2 | convolution fusion | flops 805699584 | bytes 3407872 | tf_op jit(solution)/shard_map/dot_general | solution.py:20
  7.6 4.3 %norm_m.2 = (bf16[768,1024]{1,0:T(8,128)(2,1)}, bf16[512,768]{1,0:T(8,128)(2,1)}, bf16[512,768]{1,0:T(8,128)(2,1)}) custom-call(s32[1]{0:T(128)} %bitcast.c_ref, bf16[768,1024]{1,0:T(8,128)(2,1)} %bitcast.20, f32[4,1024]{1,0:T(4,128)} %refs_11_.1), custom_call_target="tpu_custom_call" | custom-call | flops 3000000000 | bytes 4718592 | tf_op jit(solution)/shard_map/norm_m/pallas_call | solution.py:50
  11.9 1.5 multiply_sine_fusion
  13.4 19.1 %mlp_own.1 = (bf16[2048,768]{1,0:T(8,128)(2,1)}, bf16[4,768,512]{2,1,0:T(8,128)(2,1)}, bf16[768,1024]{1,0:T(8,128)(2,1)}) custom-call(bf16[768,1024]{1,0:T(8,128)(2,1)} %get-tuple-element.47.h_ref, bf16[768,1024]{1,0:T(8,128)(2,1)} %bitcast.24, bf16[1024,2048]{1,0:T(8,128)(2,1)} %wu_ref.5, bf16[2048,1024]{1,0:T(8,128)(2,1)} %wd_ref.3), custom_call_target="tpu_custom_call" | custom-call | flops 9663676416 | bytes 20971520 | tf_op jit(solution)/shard_map/mlp_own/pallas_call | solution.py:350
  32.5 6.9 %collective-permute-done.xr_ref.x_ref.refs_6_ = bf16[768,1024]{1,0:T(8,128)(2,1)S(1)} collective-permute-done((bf16[768,1024]{1,0:T(8,128)(2,1)}, bf16[768,1024]{1,0:T(8,128)(2,1)S(1)}, u32[]{:S(2)}, u32[]{:S(2)}) %collective-permute-start) | collective-permute-done | bytes 1572896 | tf_op jit(solution)/shard_map/ppermute | solution.py:765
  39.4 0.0 copy-start.1
  39.4 1.1 copy-done.1
  40.5 7.2 %norm_a.1 = (bf16[1536,1024]{1,0:T(8,128)(2,1)}, bf16[1536,512]{1,0:T(8,128)(2,1)}, bf16[1536,512]{1,0:T(8,128)(2,1)}) custom-call(s32[1]{0:T(128)} %bitcast.c_ref, bf16[768,1024]{1,0:T(8,128)(2,1)} %bitcast.21, bf16[768,1024]{1,0:T(8,128)(2,1)} %copy-done.1, f32[4,1024]{1,0:T(4,128)} %refs_11_.1), custom_call_target="tpu_custom_call" | custom-call | flops 6000000000 | bytes 9437184 | tf_op jit(solution)/shard_map/norm_a/pallas_call | solution.py:83
  47.8 0.0 copy-start
  47.8 4.5 %norm_m.3 = (bf16[768,1024]{1,0:T(8,128)(2,1)}, bf16[512,768]{1,0:T(8,128)(2,1)}, bf16[512,768]{1,0:T(8,128)(2,1)}) custom-call(s32[1]{0:T(128)} %bitcast.c_ref, bf16[768,1024]{1,0:T(8,128)(2,1)} %copy-done.1, f32[4,1024]{1,0:T(4,128)} %refs_11_.1), custom_call_target="tpu_custom_call" | custom-call | flops 3000000000 | bytes 4718592 | tf_op jit(solution)/shard_map/norm_m/pallas_call | solution.py:50
  52.3 0.0 copy-done
  52.3 8.6 %fusion.qkv_ref = bf16[1536,1536]{1,0:T(8,128)(2,1)} fusion(bf16[1536,1024]{1,0:T(8,128)(2,1)} %get-tuple-element.50, bf16[1536,1024]{1,0:T(8,128)(2,1)S(1)} %bitcast.18), kind=kOutput, calls=%fused_computation.1 | convolution fusion | flops 4834197504 | bytes 11010048 | tf_op jit(solution)/shard_map/dot_general | solution.py:20
  60.9 10.0 %mlp_pre.1 = (bf16[2048,768]{1,0:T(8,128)(2,1)}, f32[4,768,512]{2,1,0:T(8,128)}) custom-call(bf16[768,1024]{1,0:T(8,128)(2,1)} %get-tuple-element.53.h_ref, bf16[1024,2048]{1,0:T(8,128)(2,1)} %wu_ref.5), custom_call_target="tpu_custom_call" | custom-call | flops 3221225472 | bytes 16777216 | tf_op jit(solution)/shard_map/mlp_pre/pallas_call | solution.py:378
  70.9 1.4 collective-permute-done.1.dyr_ref.refs_10_
  72.4 35.3 %mlp_peer.1 = (f32[2,2,256,512]{3,2,1,0:T(8,128)}, f32[2,2,256,512]{3,2,1,0:T(8,128)}, f32[4,4,128,256]{3,2,1,0:T(8,128)}, f32[4,4,128,256]{3,2,1,0:T(8,128)}, f...) custom-call(bf16[768,1024]{1,0:T(8,128)(2,1)} %collective-permute-do, ...), custom_call_target="tpu_custom_call" | custom-call | flops 22548578304 | bytes 41943040 | tf_op jit(solution)/shard_map/mlp_peer/pallas_call | solution.py:488
  107.7 63.6 %attn.1 = (bf16[1536,1536]{1,0:T(8,128)(2,1)}, bf16[512,1536]{1,0:T(8,128)(2,1)}, f32[256,1024]{1,0:T(8,128)}, f32[2,4,128,256]{3,2,1,0:T(8,128)}, f32[2,4,128,256]{3,2,1,0:T(8,128)}) custom-call(bf16[1536,1536]{1,0:T(8,128)(2,1)} %fusion.qkv_ref, bf16[512,768]{1,0:T(8,128)(2,1)} %convolution_convert_fusion.1.dol_ref, ...), custom_call_target="tpu_custom_call" | custom-call | flops 48000000000 | bytes 8388608 | tf_op jit(solution)/shard_map/attn/pallas_call | solution.py:297
  171.3 54.3 %tail.1 = (bf16[768,1024]{1,0:T(8,128)(2,1)}, f32[4,1024]{1,0:T(4,128)}, f32[1536,128]{1,0:T(8,128)}, f32[64,1024]{1,0:T(8,128)}, f32[128,2048]{1,0:T(8,128)}) custom-call(bf16[1536,1536]{1,0:T(8,128)(2,1)} %get-tuple-element.70.refs_0_, bf16[512,1536]{1,0:T(8,128)(2,1)} %get-tuple-element.71.refs_1_, bf16[1536,512]{1,0:T(8,128)(2,1)} %get-tuple-element.51.refs_2_, ...), custom_call_target="tpu_custom_call" | custom-call | flops 40000000000 | bytes 41943040 | tf_op jit(solution)/shard_map/tail/pallas_call | solution.py:719
  225.6 3.7 %emit.1 = (bf16[768,1024]{1,0:T(8,128)(2,1)}, f32[4,1024]{1,0:T(4,128)}, f32[1536,128]{1,0:T(8,128)}, f32[64,1024]{1,0:T(8,128)}, f32[128,2048]{1,0:T(8,128)}, /*index=5*/f32[256,1024]{1,0:T(8,128)}) custom-call(bf16[768,1024]{1,0:T(8,128)(2,1)} %get-tuple-element.76.refs_0_, f32[4,1024]{1,0:T(4,128)} %get-tuple-element.77.refs_1_, ...), custom_call_target="tpu_custom_call" | custom-call | flops 1000000 | bytes 10485760 | tf_op jit(solution)/shard_map/emit/pallas_call | solution.py:747
  (2 shorter events, 0.0 us)
Async XLA Ops:
  0.6 38.8 %collective-permute-start = (bf16[768,1024]{1,0:T(8,128)(2,1)}, bf16[768,1024]{1,0:T(8,128)(2,1)S(1)}, u32[]{:S(2)}, u32[]{:S(2)}) collective-permute-start(bf16[768,1024]{1,0:T(8,128)(2,1)} %bitcast.19), channel_id=1, source_target_pairs={{0,8},{8,0},{1,9},{9,1},{2,10},{10,2},{3,11},{11,3},{4,12},{12,4},... | collective-permute-start | bytes 4718600 | tf_op jit(solution)/shard_map/ppermute | solution.py:765
  3.9 68.4 %collective-permute-start.1 = (bf16[768,1024]{1,0:T(8,128)(2,1)}, bf16[768,1024]{1,0:T(8,128)(2,1)}, u32[]{:S(2)}, u32[]{:S(2)}) collective-permute-start(bf16[768,1024]{1,0:T(8,128)(2,1)} %bitcast.23), channel_id=1, source_target_pairs={{0,8},{8,0},{1,9},{9,1},{2,10},{10,2},{3,11},{11,3},{4,12},{12,4},... | collective-permute-start | bytes 4718600 | tf_op jit(solution)/shard_map/ppermute | solution.py:765
  39.4 1.1 copy-start.1
  47.8 4.5 %copy-start = (bf16[1024,8,3,64]{0,3,2,1:T(8,128)(2,1)S(1)}, bf16[1024,8,3,64]{0,3,2,1:T(8,128)(2,1)}, u32[]{:S(2)}) copy-start(bf16[1024,8,3,64]{0,3,2,1:T(8,128)(2,1)} %param.10) | copy-start | bytes 9437188
